TPU v7x, 32 devices: a whole 2x2x4 slice. The times are simulated.
32 devices in a mesh: band: 8 (over y, x, core), field: 4 (over z).
Axes of the slice: x: 2, y: 2, z: 4, core: 2. Of those that a mesh axis runs over, the one named last changes fastest.
Arguments:
- fourier: bfloat16 [32, 192, 448], P(None, 'field', 'band'), may hold values from -6 to 6
- quad_weights: float32 [448], P('band'), may hold values from 0.1 to 1.9
- legendre: bfloat16 [32, 448, 32], P(('band', 'field')), may hold values from -0.25 to 0.25
- slot_wave: int32 [32], replicated, may hold values from 0 to 31, each once
- vert_proj: float32 [96, 96], replicated, may hold values from -0.625 to 0.625
- vert_recon: float32 [96, 96], replicated, may hold values from -0.625 to 0.625
- vert_rates: float32 [96], replicated, may hold values from 0.3 to 30
Outputs:
- spectral: bfloat16 [32, 2, 96, 32], P(('band', 'field'))
- returned: bfloat16 [32, 192, 448], P(None, 'field', 'band')
Inputs may be any that keep to these rules, and one draw needn't show every extreme that they name: `slot_wave`: every wavenumber 0 .. 31 stands in exactly one slot.
All inputs are finite; a program needn't handle non-finite values.
Results may differ from a plain program's by a relative error of at most 0.0056.
Values may be sent and summed in bfloat16 or wider, within the bound.
A program may use at most 64 MiB of HBM per device.

v0:
```python
import jax
import jax.numpy as jnp
from jax import lax
from jax.sharding import PartitionSpec as P

LEV = 96


def damping(vert_rates, total):
    order = jnp.arange(total).astype(jnp.float32)
    growth = order * (order + 1.0) / float(total * total)
    return 1.0 / (1.0 + vert_rates[:, None] * growth[None, :])


def forward_block(data, block):
    return jnp.einsum("kal,kln->kan", data, block, preferred_element_type=jnp.float32)


def forward_empty(data, block):
    return jnp.zeros((data.shape[0], data.shape[1], block.shape[2]), jnp.float32)


def pick_rows(weighted, order):
    flat = weighted.reshape(weighted.shape[0], -1)
    return flat[order].reshape(weighted.shape)


def per_device(fourier, quad_weights, legendre, slot_wave, vert_proj, vert_recon, vert_rates):
    n_field = lax.axis_size("field")
    per_dev = legendre.shape[0]
    nlat = legendre.shape[1]
    total = legendre.shape[2]
    weighted = (fourier.astype(jnp.float32) * quad_weights).astype(jnp.bfloat16)
    moved = lax.all_to_all(
        lax.all_to_all(
            pick_rows(weighted, slot_wave), "band", split_axis=0, concat_axis=2, tiled=True
        ),
        "field",
        split_axis=0,
        concat_axis=1,
        tiled=True,
    )
    me = lax.axis_index("band") * n_field + lax.axis_index("field")
    my_waves = lax.dynamic_slice_in_dim(slot_wave, me * per_dev, per_dev)
    width = min(128, total)
    lowest = jnp.min(my_waves)
    pieces = []
    for start in range(0, total, width):
        block = legendre[:, :, start : start + width]
        pieces.append(
            lax.cond(
                start + block.shape[2] > lowest,
                lambda blk: forward_block(moved, blk),
                lambda blk: forward_empty(moved, blk),
                block,
            )
        )
    direct = jnp.concatenate(pieces, axis=2)
    gamma = damping(vert_rates, total)
    direct = direct.reshape(per_dev, 2, LEV, total)
    modes = jnp.einsum("jl,kcln->kcjn", vert_proj, direct, precision=lax.Precision.HIGHEST) * gamma
    solved = jnp.einsum("lj,kcjn->kcln", vert_recon, modes, precision=lax.Precision.HIGHEST)
    keep = (jnp.arange(total)[None, :] >= my_waves[:, None]).astype(jnp.float32)
    spectral = (solved * keep[:, None, None, :]).astype(jnp.bfloat16)
    flat = spectral.reshape(per_dev, 2 * LEV, total)
    back = jnp.zeros((per_dev, 2 * LEV, nlat), jnp.float32)
    for start in range(0, total, width):
        block = legendre[:, :, start : start + width]
        coeffs = flat[:, :, start : start + width]
        back = back + lax.cond(
            start + block.shape[2] > lowest,
            lambda pair: jnp.einsum(
                "kan,kln->kal", pair[0], pair[1], preferred_element_type=jnp.float32
            ),
            lambda pair: jnp.zeros((per_dev, 2 * LEV, nlat), jnp.float32),
            (coeffs, block),
        )
    back = back.astype(jnp.bfloat16)
    slots = jnp.arange(total)
    inverse = jnp.zeros((total,), jnp.int32).at[slot_wave].set(slots)
    first_back = lax.all_to_all(back, "field", split_axis=1, concat_axis=0, tiled=True)
    arrived = lax.all_to_all(first_back, "band", split_axis=2, concat_axis=0, tiled=True)
    returned = pick_rows(arrived, inverse)
    return (spectral, returned)


def solution(mesh):
    placed = (
        P(None, "field", "band"),
        P("band"),
        P(("band", "field"), None, None),
        P(),
        P(),
        P(),
        P(),
    )
    return jax.shard_map(
        per_device,
        mesh=mesh,
        in_specs=placed,
        out_specs=(P(("band", "field"), None, None, None), P(None, "field", "band")),
        check_vma=False,
    )
```

profile of v0, /device:TPU:0, one launch (start us, length us, event | category | flops | bytes accessed | tf_op | source)
XLA Modules:
  0.0 60.8 jit_solution(2012786956487332678)
XLA Ops:
  0.6 0.7 %compare_select_fusion.1 = s32[32]{0:T(128)S(1)} fusion(s32[32]{0:T(128)} %param.14), kind=kLoop, calls=%fused_computation.22 | loop fusion | flops 96 | bytes 256 | tf_op jit(solution)/shard_map/select_n | solution.py:25
  1.3 0.6 %copy-done.5 = f32[56]{0:T(128)S(1)} copy-done((f32[56]{0:T(128)S(1)}, f32[56]{0:T(128)}, u32[]{:S(2)}) %copy-start.5) | copy-done | bytes 248
  2.0 1.1 %multiply_convert_fusion = bf16[32,48,56]{2,1,0:T(8,128)(2,1)S(1)} fusion(bf16[32,48,56]{2,1,0:T(8,128)(2,1)} %param.11, f32[56]{0:T(128)S(1)} %copy-done.5), kind=kLoop, calls=%fused_computation.14 | loop fusion | flops 258048 | bytes 344288 | tf_op jit(solution)/shard_map/convert_element_type | solution.py:33
  3.0 0.4 reshape.104
  3.4 0.7 %gather_fusion = bf16[32,2688]{1,0:T(8,128)(2,1)S(1)} fusion(bf16[32,2688]{1,0:T(8,128)(2,1)S(1)} %reshape.104, s32[1024]{0:T(1024)S(1)} %pad_clamp_fusion.1), kind=kCustom, calls=%fused_computation | custom fusion | bytes 344192 | tf_op jit(solution)/shard_map/gather | solution.py:25
  4.1 0.6 %reshape.105 = bf16[32,48,56]{2,1,0:T(8,128)(2,1)S(1)} reshape(bf16[32,2688]{1,0:T(8,128)(2,1)S(1)} %gather_fusion) | data formatting | bytes 344064 | tf_op jit(solution)/shard_map/reshape | solution.py:25
  4.7 1.3 %reshape.141 = bf16[8,2,5376]{2,1,0:T(2,128)(2,1)} reshape(bf16[32,48,56]{2,1,0:T(8,128)(2,1)S(1)} %reshape.105) | data formatting | bytes 344064
  6.1 5.2 %all-to-all-start = ((bf16[8,2,5376]{2,1,0:T(2,128)(2,1)}), bf16[8,2,5376]{2,1,0:T(2,128)(2,1)S(1)}, u32[]{:S(2)}, u32[]{:S(2)}) async-start(bf16[8,2,5376]{2,1,0:T(2,128)(2,1)} %reshape.141), calls=%async_computation | async-start | bytes 344064 | tf_op jit(solution)/shard_map/all_to_all | solution.py:35
  11.3 0.7 %copy-done.6 = s32[32]{0:T(128)S(1)} copy-done((s32[32]{0:T(128)S(1)}, s32[32]{0:T(128)}, u32[]{:S(2)}) %copy-start.6) | copy-done | bytes 152
  11.9 0.6 dynamic_slice.3
  12.5 4.7 %all-to-all-done = bf16[8,2,5376]{2,1,0:T(2,128)(2,1)S(1)} async-done(((bf16[8,2,5376]{2,1,0:T(2,128)(2,1)}), bf16[8,2,5376]{2,1,0:T(2,128)(2,1)S(1)}, u32[]{:S(2)}, u32[]{:S(2)}) %all-to-all-start) | async-done | bytes 172064 | tf_op jit(solution)/shard_map/all_to_all | solution.py:35
  17.2 0.7 %reshape.142 = bf16[32,48,56]{2,1,0:T(8,128)(2,1)S(1)} reshape(bf16[8,2,5376]{2,1,0:T(2,128)(2,1)S(1)} %all-to-all-done) | data formatting | bytes 344064
  18.1 1.0 %all_to_all.44 = bf16[4,48,448]{2,1,0:T(8,128)(2,1)} reshape(bf16[4,48,8,56]{3,2,1,0:T(8,128)(2,1)S(1)} %bitcast.64) | data formatting | bytes 344064 | tf_op jit(solution)/shard_map/all_to_all | solution.py:35
  19.1 5.0 %all-to-all-start.1 = ((bf16[4,48,448]{2,1,0:T(8,128)(2,1)}), bf16[4,48,448]{2,1,0:T(8,128)(2,1)S(1)}, u32[]{:S(2)}, u32[]{:S(2)}) async-start(bf16[4,48,448]{2,1,0:T(8,128)(2,1)} %all_to_all.44), calls=%async_computation.1 | async-start | bytes 393216 | tf_op jit(solution)/shard_map/all_to_all | solution.py:34
  24.1 0.6 %compare_convert_fusion = f32[32]{0:T(128)S(1)} fusion(s32[]{:T(128)} %bitcast.6), kind=kLoop, calls=%fused_computation.23 | loop fusion | flops 64 | bytes 132 | tf_op jit(solution)/shard_map/convert_element_type | solution.py:63
  25.4 0.6 %copy-done.4 = f32[96]{0:T(128)S(1)} copy-done((f32[96]{0:T(128)S(1)}, f32[96]{0:T(128)}, u32[]{:S(2)}) %copy-start.4) | copy-done | bytes 408
  26.1 5.3 %all-to-all-done.1 = bf16[4,48,448]{2,1,0:T(8,128)(2,1)S(1)} async-done(((bf16[4,48,448]{2,1,0:T(8,128)(2,1)}), bf16[4,48,448]{2,1,0:T(8,128)(2,1)S(1)}, u32[]{:S(2)}, u32[]{:S(2)}) %all-to-all-start.1) | async-done | bytes 172064 | tf_op jit(solution)/shard_map/all_to_all | solution.py:34
  31.8 0.6 copy-done.3
  32.6 0.6 copy-done.2
  33.9 0.5 broadcast.81
  34.4 1.9 %reduce = bf16[192,448]{1,0:T(8,128)(2,1)S(1)} reduce(bf16[192,1,448]{2,1,0:T(2,128)(2,1)S(1)} %bitcast.66, bf16[]{:T(256)} %broadcast.81), dimensions={1}, to_apply=%bitcast.60.reduce_sub_computation | reduce | bytes 344066
  36.2 0.9 %reshape.143 = bf16[4,2,10752]{2,1,0:T(2,128)(2,1)} reshape(bf16[192,448]{1,0:T(8,128)(2,1)S(1)} %reduce) | data formatting | bytes 344064
  37.2 3.4 %all-to-all-start.2 = ((bf16[4,2,10752]{2,1,0:T(2,128)(2,1)}), bf16[4,2,10752]{2,1,0:T(2,128)(2,1)S(1)}, u32[]{:S(2)}, u32[]{:S(2)}) async-start(bf16[4,2,10752]{2,1,0:T(2,128)(2,1)} %reshape.143), calls=%async_computation.2 | async-start | bytes 344064 | tf_op jit(solution)/shard_map/all_to_all | solution.py:81
  40.5 0.7 %scatter_custom_fusion = s32[32]{0:T(128)S(1)} fusion(s32[32]{0:T(128)S(1)} %compare_select_fusion.1, s32[32]{0:T(128)S(1)} %iota.16, s32[]{:T(128)} %constant.6.clone.1), kind=kCustom, calls=%fused_computation.26 | custom fusion | bytes 132 | tf_op jit(solution)/shard_map/scatter | solution.py:80
  41.2 5.3 %all-to-all-done.2 = bf16[4,2,10752]{2,1,0:T(2,128)(2,1)S(1)} async-done(((bf16[4,2,10752]{2,1,0:T(2,128)(2,1)}), bf16[4,2,10752]{2,1,0:T(2,128)(2,1)S(1)}, u32[]{:S(2)}, u32[]{:S(2)}) %all-to-all-start.2) | async-done | bytes 172064 | tf_op jit(solution)/shard_map/all_to_all | solution.py:81
  47.1 1.3 %reshape.145 = bf16[8,2,5376]{2,1,0:T(2,128)(2,1)} reshape(bf16[448,4,48]{2,1,0:T(4,128)(2,1)S(1)} %bitcast.61) | data formatting | bytes 344064
  48.4 3.4 %all-to-all-start.3 = ((bf16[8,2,5376]{2,1,0:T(2,128)(2,1)}), bf16[8,2,5376]{2,1,0:T(2,128)(2,1)S(1)}, u32[]{:S(2)}, u32[]{:S(2)}) async-start(bf16[8,2,5376]{2,1,0:T(2,128)(2,1)} %reshape.145), calls=%async_computation.3 | async-start | bytes 344064 | tf_op jit(solution)/shard_map/all_to_all | solution.py:82
  51.8 5.8 %all-to-all-done.3 = bf16[8,2,5376]{2,1,0:T(2,128)(2,1)S(1)} async-done(((bf16[8,2,5376]{2,1,0:T(2,128)(2,1)}), bf16[8,2,5376]{2,1,0:T(2,128)(2,1)S(1)}, u32[]{:S(2)}, u32[]{:S(2)}) %all-to-all-start.3) | async-done | bytes 172064 | tf_op jit(solution)/shard_map/all_to_all | solution.py:82
  57.6 0.5 reshape.146
  58.4 0.4 reshape.107
  58.8 0.7 %gather_fusion.1 = bf16[32,2688]{1,0:T(8,128)(2,1)S(1)} fusion(bf16[32,2688]{1,0:T(8,128)(2,1)S(1)} %reshape.107, s32[1024]{0:T(1024)S(1)} %pad_clamp_fusion), kind=kCustom, calls=%fused_computation.1 | custom fusion | bytes 344192 | tf_op jit(solution)/shard_map/gather | solution.py:25
  59.4 1.4 %reshape.108 = bf16[32,48,56]{2,1,0:T(8,128)(2,1)} reshape(bf16[32,2688]{1,0:T(8,128)(2,1)S(1)} %gather_fusion.1) | data formatting | bytes 344064 | tf_op jit(solution)/shard_map/reshape | solution.py:25
  (28 shorter events, 2.9 us)
Async XLA Ops:
  0.6 31.0 %copy-start = (f32[96,96]{1,0:T(8,128)S(1)}, f32[96,96]{1,0:T(8,128)}, u32[]{:S(2)}) copy-start(f32[96,96]{1,0:T(8,128)} %param.15) | copy-start | bytes 110596
  1.3 0.7 %copy-start.5 = (f32[56]{0:T(128)S(1)}, f32[56]{0:T(128)}, u32[]{:S(2)}) copy-start(f32[56]{0:T(128)} %param.12) | copy-start | bytes 676
  6.1 11.1 %all-to-all-start = ((bf16[8,2,5376]{2,1,0:T(2,128)(2,1)}), bf16[8,2,5376]{2,1,0:T(2,128)(2,1)S(1)}, u32[]{:S(2)}, u32[]{:S(2)}) async-start(bf16[8,2,5376]{2,1,0:T(2,128)(2,1)} %reshape.141), calls=%async_computation | async-start | bytes 344064 | tf_op jit(solution)/shard_map/all_to_all | solution.py:35
  11.3 0.7 %copy-start.6 = (s32[32]{0:T(128)S(1)}, s32[32]{0:T(128)}, u32[]{:S(2)}) copy-start(s32[32]{0:T(128)} %param.14) | copy-start | bytes 388
  19.1 12.3 %copy-start.1 = (bf16[1,448,32]{1,2,0:T(8,128)(2,1)S(1)}, bf16[1,448,32]{1,2,0:T(8,128)(2,1)}, u32[]{:S(2)}) copy-start(bf16[1,448,32]{1,2,0:T(8,128)(2,1)} %param.13) | copy-start | bytes 86020
  19.1 12.3 %all-to-all-start.1 = ((bf16[4,48,448]{2,1,0:T(8,128)(2,1)}), bf16[4,48,448]{2,1,0:T(8,128)(2,1)S(1)}, u32[]{:S(2)}, u32[]{:S(2)}) async-start(bf16[4,48,448]{2,1,0:T(8,128)(2,1)} %all_to_all.44), calls=%async_computation.1 | async-start | bytes 393216 | tf_op jit(solution)/shard_map/all_to_all | solution.py:34
  25.4 0.7 %copy-start.4 = (f32[96]{0:T(128)S(1)}, f32[96]{0:T(128)}, u32[]{:S(2)}) copy-start(f32[96]{0:T(128)} %param.17) | copy-start | bytes 1156
  31.6 0.8 %copy-start.3 = (f32[96,96]{1,0:T(8,128)S(1)}, f32[96,96]{1,0:T(8,128)}, u32[]{:S(2)}) copy-start(f32[96,96]{1,0:T(8,128)} %param.16) | copy-start | bytes 110596
  32.6 0.6 copy-start.2
  37.2 9.4 %all-to-all-start.2 = ((bf16[4,2,10752]{2,1,0:T(2,128)(2,1)}), bf16[4,2,10752]{2,1,0:T(2,128)(2,1)S(1)}, u32[]{:S(2)}, u32[]{:S(2)}) async-start(bf16[4,2,10752]{2,1,0:T(2,128)(2,1)} %reshape.143), calls=%async_computation.2 | async-start | bytes 344064 | tf_op jit(solution)/shard_map/all_to_all | solution.py:81
  48.4 9.3 %all-to-all-start.3 = ((bf16[8,2,5376]{2,1,0:T(2,128)(2,1)}), bf16[8,2,5376]{2,1,0:T(2,128)(2,1)S(1)}, u32[]{:S(2)}, u32[]{:S(2)}) async-start(bf16[8,2,5376]{2,1,0:T(2,128)(2,1)} %reshape.145), calls=%async_computation.3 | async-start | bytes 344064 | tf_op jit(solution)/shard_map/all_to_all | solution.py:82
where the time goes:
time: 61.6 us; the launch traced here: 60.8 us
  waiting for transfers between devices  21.1 us (34%)
  starting transfers between devices  16.9 us (27%)
  local copies, waits for them, and re-layouts  16.1 us (26%)
  other arithmetic  4.35 us (7%)
  between operations  1.5 us (2%)
  matrix products  0.79 us (1%)
    unnamed x22, local copies, waits for them, and re-layouts  8.56 us
    all_to_all x1, waiting for transfers between devices, per_device(): lax.all_to_all(first_back, 'band', split_axis=2, concat_axis=0, tiled=True)  5.85 us
    all_to_all x1, waiting for transfers between devices, per_device(): lax.all_to_all(back, 'field', split_axis=1, concat_axis=0, tiled=True)  5.32 us
    all_to_all x1, waiting for transfers between devices, per_device(): lax.all_to_all(lax.all_to_all(pick_rows(weighted, slot_wave), 'band', spl...  5.27 us
    all_to_all x1, starting transfers between devices, per_device(): lax.all_to_all(pick_rows(weighted, slot_wave), 'band', split_axis=0, conc...  5.2 us
    all_to_all x1, starting transfers between devices, per_device(): lax.all_to_all(lax.all_to_all(pick_rows(weighted, slot_wave), 'band', spl...  5 us
    all_to_all x1, waiting for transfers between devices, per_device(): lax.all_to_all(pick_rows(weighted, slot_wave), 'band', split_axis=0, conc...  4.69 us
    all_to_all x1, starting transfers between devices, per_device(): lax.all_to_all(first_back, 'band', split_axis=2, concat_axis=0, tiled=True)  3.38 us
  transfers between devices with their start and end apart: 4, of which 4 were waited for; matrix products, arithmetic and copies ran while one was open for 3% of the time, Pallas kernels for 0%

commit v1 on v0

v1 whole, which is shorter than its diff:
```python
import functools

import jax
import jax.numpy as jnp
from jax import lax
from jax.experimental import pallas as pl
from jax.experimental.pallas import tpu as pltpu
from jax.sharding import PartitionSpec as P

LEV = 96
LANES = 128
MESH = pl.DeviceIdType.MESH


def exchange(
    nb, nf, pack, wave_ref, quad_ref, rates_ref, leg_ref, proj_ref, recon_ref, fourier_ref,
    spec_ref, back_ref,
    four_v, send_a, recv_a, send_b, table, acc, four_sem, send_a_sem, recv_a_sem, send_b_sem, recv_b_sem,
):
    n_dev = nb * nf
    my_b, my_f = lax.axis_index("band"), lax.axis_index("field")
    me = my_b * nf + my_f
    rows, width = fourier_ref.shape[1], fourier_ref.shape[2]
    part = rows // pack
    total = leg_ref.shape[2]

    def peer(step):
        other = lax.rem(me + step, n_dev)
        return other, (other // nf, lax.rem(other, nf))

    fetch = pltpu.make_async_copy(fourier_ref, four_v, four_sem)
    fetch.start()
    barrier = pltpu.get_barrier_semaphore()

    @pl.loop(1, n_dev)
    def _(step):
        pl.semaphore_signal(barrier, inc=1, device_id=peer(step)[1], device_id_type=MESH)

    @pl.loop(0, nb)
    def _(b):
        block = leg_ref[0, pl.ds(pl.multiple_of(b * width, 8), width), :].astype(jnp.float32)
        pieces = []
        for h in range(pack):
            line = [jnp.zeros((width, total), jnp.float32)] * pack
            line[h] = block
            pieces.append(jnp.concatenate(line, axis=1) if pack > 1 else block)
        pieces.append(jnp.zeros((LANES - pack * width, pack * total), jnp.float32))
        table[b] = jnp.concatenate(pieces, axis=0).astype(jnp.bfloat16)

    fetch.wait()
    quad = quad_ref[...]

    @pl.loop(0, n_dev)
    def _(s):
        x = (four_v[wave_ref[s]].astype(jnp.float32) * quad)
        pieces = [x[h * part : (h + 1) * part] for h in range(pack)]
        pieces.append(jnp.zeros((part, LANES - pack * width), jnp.float32))
        send_a[s] = jnp.concatenate(pieces, axis=1).astype(jnp.bfloat16)

    pl.semaphore_wait(barrier, n_dev - 1)

    own_a = pltpu.make_async_copy(send_a.at[me], recv_a.at[my_b, my_f], recv_a_sem.at[my_b])
    own_a.start()

    @pl.loop(1, n_dev)
    def _(step):
        other, where = peer(step)
        pltpu.make_async_remote_copy(
            src_ref=send_a.at[other],
            dst_ref=recv_a.at[my_b, my_f],
            send_sem=send_a_sem,
            recv_sem=recv_a_sem.at[my_b],
            device_id=where,
            device_id_type=MESH,
        ).start()

    eye = lax.broadcasted_iota(jnp.int32, (LEV, LEV), 0) == lax.broadcasted_iota(jnp.int32, (LEV, LEV), 1)
    rates = jnp.sum(jnp.where(eye, rates_ref[...], 0.0), axis=1, keepdims=True)
    degree = lax.broadcasted_iota(jnp.int32, (1, 2 * total), 1)
    degree = jnp.where(degree >= total, degree - total, degree)
    order = degree.astype(jnp.float32)
    gamma = 1.0 / (1.0 + rates * (order * (order + 1.0) / float(total * total)))
    keep = (degree >= wave_ref[me]).astype(jnp.float32)

    acc[...] = jnp.zeros_like(acc)

    @pl.loop(0, nb)
    def _(step):
        b = lax.rem(my_b + step, nb)
        pltpu.make_async_copy(recv_a.at[b], recv_a.at[b], recv_a_sem.at[b]).wait()
        data = recv_a[b].reshape(nf * part, LANES)
        acc[...] += jnp.dot(data, table[b], preferred_element_type=jnp.float32)

    per_c = nf * pack // 2
    group = [acc[(g // pack) * part : (g // pack + 1) * part, (g % pack) * total : (g % pack + 1) * total]
             for g in range(nf * pack)]
    direct = jnp.concatenate(
        [jnp.concatenate(group[c * per_c : (c + 1) * per_c], axis=0) for c in range(2)], axis=1
    )
    exact = dict(preferred_element_type=jnp.float32, precision=lax.Precision.HIGHEST)
    modes = jnp.dot(proj_ref[...], direct, **exact) * gamma
    solved = jnp.dot(recon_ref[...], modes, **exact) * keep
    for c in range(2):
        spec_ref[c] = solved[:, c * total : (c + 1) * total].astype(jnp.bfloat16)

    def piece(g):
        c, l = g // per_c, (g % per_c) * part
        return solved[l : l + part, c * total : (c + 1) * total]

    packed = jnp.concatenate(
        [jnp.concatenate([piece(f * pack + h) for h in range(pack)], axis=1) for f in range(nf)], axis=0
    ).astype(jnp.bfloat16)

    @pl.loop(0, nb)
    def _(b):
        out = lax.dot_general(packed, table[b], (((1,), (1,)), ((), ())), preferred_element_type=jnp.float32)
        send_b[pl.ds(b * nf, nf)] = out.astype(jnp.bfloat16).reshape(nf, part, LANES)

    own_b = pltpu.make_async_copy(send_b.at[me], back_ref.at[me], recv_b_sem)
    own_b.start()

    @pl.loop(1, n_dev)
    def _(step):
        other, where = peer(step)
        pltpu.make_async_remote_copy(
            src_ref=send_b.at[other],
            dst_ref=back_ref.at[me],
            send_sem=send_b_sem,
            recv_sem=recv_b_sem,
            device_id=where,
            device_id_type=MESH,
        ).start()

    pltpu.make_async_copy(back_ref, back_ref, recv_b_sem).wait()
    others = pl.ds(0, n_dev - 1)
    pltpu.make_async_copy(send_a.at[others], send_a.at[others], send_a_sem).wait()
    pltpu.make_async_copy(send_b.at[others], send_b.at[others], send_b_sem).wait()


def unpack(pack, wave_ref, back_ref, spec_in, spec_out, out_ref):
    part = back_ref.shape[1]
    width = out_ref.shape[2]
    spec_out[0] = spec_in[...]

    @pl.loop(0, back_ref.shape[0])
    def _(s):
        w = wave_ref[s]
        x = back_ref[s].astype(jnp.float32)
        for h in range(pack):
            out_ref[w, h * part : (h + 1) * part, :] = x[:, h * width : (h + 1) * width].astype(jnp.bfloat16)


def per_device(fourier, quad_weights, legendre, slot_wave, vert_proj, vert_recon, vert_rates):
    nb, nf = lax.axis_size("band"), lax.axis_size("field")
    n_dev = nb * nf
    waves, rows, width = fourier.shape
    per_dev, nlat, total = legendre.shape
    assert per_dev == 1 and waves == n_dev and nlat == nb * width and width <= LANES
    pack = 1
    while rows % (2 * pack * 8) == 0 and 2 * pack * width <= LANES and 2 * pack * total <= LANES:
        pack *= 2
    part = rows // pack
    vmem = pl.BlockSpec(memory_space=pltpu.VMEM)
    smem = pl.BlockSpec(memory_space=pltpu.SMEM)
    anywhere = pl.BlockSpec(memory_space=pl.ANY)
    blocks = (n_dev, part, LANES)
    spec, back = pl.pallas_call(
        functools.partial(exchange, nb, nf, pack),
        out_shape=(
            jax.ShapeDtypeStruct((2, LEV, total), jnp.bfloat16),
            jax.ShapeDtypeStruct(blocks, jnp.bfloat16),
        ),
        in_specs=[smem, vmem, vmem, vmem, vmem, vmem, anywhere],
        out_specs=(vmem, vmem),
        scratch_shapes=[
            pltpu.VMEM(fourier.shape, jnp.bfloat16),
            pltpu.VMEM(blocks, jnp.bfloat16),
            pltpu.VMEM((nb, nf, part, LANES), jnp.bfloat16),
            pltpu.VMEM(blocks, jnp.bfloat16),
            pltpu.VMEM((nb, LANES, pack * total), jnp.bfloat16),
            pltpu.VMEM((nf * part, pack * total), jnp.float32),
            pltpu.SemaphoreType.DMA,
            pltpu.SemaphoreType.DMA,
            pltpu.SemaphoreType.DMA((nb,)),
            pltpu.SemaphoreType.DMA,
            pltpu.SemaphoreType.DMA,
        ],
        compiler_params=pltpu.CompilerParams(collective_id=0, has_side_effects=True),
    )(slot_wave, quad_weights[None], vert_rates[None], legendre, vert_proj, vert_recon, fourier)
    spectral, returned = pl.pallas_call(
        functools.partial(unpack, pack),
        out_shape=(
            jax.ShapeDtypeStruct((1, 2, LEV, total), jnp.bfloat16),
            jax.ShapeDtypeStruct(fourier.shape, jnp.bfloat16),
        ),
        in_specs=[smem, vmem, vmem],
        out_specs=(vmem, vmem),
    )(slot_wave, back, spec)
    return spectral, returned


def solution(mesh):
    placed = (
        P(None, "field", "band"),
        P("band"),
        P(("band", "field"), None, None),
        P(),
        P(),
        P(),
        P(),
    )
    return jax.shard_map(
        per_device,
        mesh=mesh,
        in_specs=placed,
        out_specs=(P(("band", "field"), None, None, None), P(None, "field", "band")),
        check_vma=False,
    )
```

time: 61.6 us -> 32.4 us (0.53)
  Pallas kernels: 0 us -> 28.5 us
  waiting for transfers between devices: 21.1 us -> 0 us
  starting transfers between devices: 16.9 us -> 0 us
  local copies, waits for them, and re-layouts: 16.1 us -> 3 us
  other arithmetic: 4.35 us -> 0 us
  between operations: 1.5 us -> 0.64 us
  matrix products: 0.79 us -> 0 us
    pallas_call x0 -> x2, Pallas kernels: none -> 28.5 us  [the longest x1 24.5 us: per_device(): pl.pallas_call(functools.partial(exchange, nb, nf, pack), out_shape=(jax....]
    all_to_all x4 -> x0, waiting for transfers between devices: 21.1 us -> none  [the longest x1 5.85 us: per_device(): lax.all_to_all(first_back, 'band', split_axis=2, concat_axis=0, tiled=True)]
    all_to_all x4 -> x0, starting transfers between devices: 16.9 us -> none  [the longest x1 5.2 us: per_device(): lax.all_to_all(pick_rows(weighted, slot_wave), 'band', split_axis=0, conc...]
    unnamed x22 -> x1, local copies, waits for them, and re-layouts: 8.56 us -> 1.52 us
    reshape x4 -> x0, local copies, waits for them, and re-layouts: 2.76 us -> none  [the longest x2 2.03 us: pick_rows(): return flat[order].reshape(weighted.shape)]
    unnamed x1 -> x0, other arithmetic: 1.87 us -> none
    all_to_all x4 -> x0, local copies, waits for them, and re-layouts: 1.77 us -> none  [the longest x2 1.22 us: per_device(): lax.all_to_all(pick_rows(weighted, slot_wave), 'band', split_axis=0, conc...]
    convert_element_type x2 -> x0, other arithmetic: 1.72 us -> none  [the longest x1 1.07 us: per_device(): weighted = (fourier.astype(jnp.float32) * quad_weights).astype(jnp.bfloat16)]
  transfers between devices with their start and end apart: 4 -> 0, of which waited for: 4 -> 0; matrix products, arithmetic and copies ran while one was open for 3% -> 0% of each run, Pallas kernels for 0% -> 0%
where the time goes in v1:
time: 32.4 us; the launch traced here: 32.1 us
  Pallas kernels  28.5 us (88%)
  local copies, waits for them, and re-layouts  3 us (9%)
  between operations  0.64 us (2%)
    pallas_call x1, Pallas kernels, per_device(): pl.pallas_call(functools.partial(exchange, nb, nf, pack), out_shape=(jax....  24.5 us
    pallas_call x1, Pallas kernels, per_device(): pl.pallas_call(functools.partial(unpack, pack), out_shape=(jax.ShapeDtype...  3.97 us
    unnamed x1, local copies, waits for them, and re-layouts  1.52 us
    pallas_call x1, local copies, waits for them, and re-layouts, per_device(): pl.pallas_call(functools.partial(unpack, pack), out_shape=(jax.ShapeDtype...  1.48 us

profile of v1, /device:TPU:0, one launch (start us, length us, event | category | flops | bytes accessed | tf_op | source)
XLA Modules:
  0.0 32.1 jit_solution(1149565169852036682)
XLA Ops:
  0.6 1.5 %copy.9.leg_ref = bf16[1,448,32]{2,1,0:T(8,128)(2,1)} copy(bf16[1,448,32]{1,2,0:T(8,128)(2,1)} %param.9) | data formatting | bytes 57344 | tf_op args[2]
  2.2 24.5 %shard_map.86 = (bf16[2,96,32]{2,1,0:T(8,128)(2,1)}, bf16[32,24,128]{2,1,0:T(8,128)(2,1)}) custom-call(s32[32]{0:T(128)} %wave_ref.3, f32[1,56]{1,0:T(1,128)} %bitcast.2, f32[1,96]{1,0:T(1,128)} %bitcast.3, bf16[1,448,32]{2,1,0:T(8,128)(2,1)} %copy.9.leg_ref, f32[96,96]{1,0:T(8,128)} %proj_ref.1, f32[96,96]{1,0:T(8,128)} %recon_ref.1, ...), custom_call_target="tpu_custom_call" | custom-call | tf_op jit(solution)/shard_map/pallas_call | solution.py:167
  26.7 4.0 %shard_map.87 = (bf16[1,2,96,32]{3,2,1,0:T(8,128)(2,1)}, bf16[32,48,56]{2,1,0:T(8,128)(2,1)}) custom-call(s32[32]{0:T(128)} %wave_ref.3, bf16[32,24,128]{2,1,0:T(8,128)(2,1)} %get-tuple-element.4.back_ref, bf16[2,96,32]{2,1,0:T(8,128)(2,1)} %get-tuple-element.5.spec_in), custom_call_target="tpu_custom_call" | custom-call | tf_op jit(solution)/shard_map/pallas_call | solution.py:190
  30.6 1.5 %copy.10 = bf16[1,2,96,32]{2,3,1,0:T(8,128)(2,1)} copy(bf16[1,2,96,32]{3,2,1,0:T(8,128)(2,1)} %get-tuple-element.6) | data formatting | bytes 24576 | tf_op jit(solution)/shard_map/pallas_call | solution.py:190

commit v2 on v1

v2 whole, which is shorter than its diff:
```python
import functools

import jax
import jax.numpy as jnp
from jax import lax
from jax.experimental import pallas as pl
from jax.experimental.pallas import tpu as pltpu
from jax.sharding import PartitionSpec as P

LEV = 96
LANES = 128
UNROLL = 4
CHUNKS = 4
VMEM_LIMIT = 60 * 1024 * 1024
MESH = pl.DeviceIdType.MESH


def exchange(
    nb, nf, pack, wave_hbm, row_hbm, quad_hbm, rates_hbm, leg_hbm, proj_hbm, recon_hbm, fourier_hbm,
    spec_ref, out_ref,
    wave, order, row, quad, rates, leg, proj, recon, four, send_a, recv_a, send_b, recv_b, table, acc,
    inverse_v, spec_v, out_v,
    small_sem, four_sem, out_sem, send_a_sem, recv_a_sem, send_b_sem, recv_b_sem,
):
    n_dev = nb * nf
    my_b, my_f = lax.axis_index("band"), lax.axis_index("field")
    me = my_b * nf + my_f
    rows, width = four.shape[1], four.shape[2]
    part = rows // pack
    total = leg.shape[1]

    def peer(step):
        other = lax.rem(me + step, n_dev)
        return other, (other // nf, lax.rem(other, nf))

    barrier = pltpu.get_barrier_semaphore()

    @pl.loop(1, n_dev, unroll=UNROLL)
    def _(step):
        pl.semaphore_signal(barrier, inc=1, device_id=peer(step)[1], device_id_type=MESH)

    pairs = ((wave_hbm, wave), (quad_hbm, quad), (row_hbm, row), (leg_hbm, leg), (rates_hbm, rates),
             (proj_hbm, proj), (recon_hbm, recon))
    loads = [pltpu.make_async_copy(a, b, small_sem.at[i]) for i, (a, b) in enumerate(pairs)]
    fetch = pltpu.make_async_copy(fourier_hbm, four, four_sem)
    loads[0].start()
    loads[1].start()
    fetch.start()
    for load in loads[2:]:
        load.start()
    loads[0].wait()
    loads[1].wait()
    fetch.wait()

    @pl.loop(0, n_dev, unroll=UNROLL)
    def _(s):
        x = four[jnp.clip(wave[s], 0, n_dev - 1)].astype(jnp.float32) * quad[...]
        pieces = [x[h * part : (h + 1) * part] for h in range(pack)]
        pieces.append(jnp.zeros((part, LANES - pack * width), jnp.float32))
        send_a[s] = jnp.concatenate(pieces, axis=1).astype(jnp.bfloat16)

    pl.semaphore_wait(barrier, n_dev - 1)

    @pl.loop(1, n_dev, unroll=UNROLL)
    def _(step):
        other, where = peer(step)
        pltpu.make_async_remote_copy(
            src_ref=send_a.at[other],
            dst_ref=recv_a.at[my_b, my_f],
            send_sem=send_a_sem,
            recv_sem=recv_a_sem.at[my_b],
            device_id=where,
            device_id_type=MESH,
        ).start()

    pltpu.make_async_copy(send_a.at[me], recv_a.at[my_b, my_f], recv_a_sem.at[my_b]).start()

    loads[2].wait()
    down = lax.broadcasted_iota(jnp.int32, (n_dev, n_dev), 0)
    across = lax.broadcasted_iota(jnp.int32, (n_dev, n_dev), 1)
    aim = lax.broadcasted_iota(jnp.int32, (n_dev, inverse_v.shape[1]), 1)
    source = lax.broadcasted_iota(jnp.int32, (n_dev, inverse_v.shape[1]), 0)
    column = jnp.sum(jnp.where(down == across, row[...].astype(jnp.float32), 0.0), axis=1, keepdims=True)
    hit = column.astype(jnp.int32) == aim
    inverse_v[...] = jnp.sum(jnp.where(hit, source.astype(jnp.float32), 0.0), axis=0, keepdims=True).astype(jnp.int32)

    loads[3].wait()
    for b in range(nb):
        block = leg[0, :, b * width : (b + 1) * width].astype(jnp.float32)
        lines = []
        for h in range(pack):
            line = [jnp.zeros((total, h * width), jnp.float32)] if h else []
            line += [block, jnp.zeros((total, LANES - (h + 1) * width), jnp.float32)]
            lines.append(jnp.concatenate(line, axis=1))
        table[b] = jnp.concatenate(lines, axis=0).astype(jnp.bfloat16)

    to_scalar = pltpu.make_async_copy(inverse_v, order, small_sem.at[2])
    to_scalar.start()
    for load in loads[4:]:
        load.wait()
    degree = lax.broadcasted_iota(jnp.int32, (2 * total, 1), 0)
    degree = jnp.where(degree >= total, degree - total, degree)
    level = degree.astype(jnp.float32)
    gamma = 1.0 / (1.0 + rates[...] * (level * (level + 1.0) / float(total * total)))
    keep = (degree >= wave[me]).astype(jnp.float32)
    to_scalar.wait()

    acc[...] = jnp.zeros_like(acc)

    across_rows = (((1,), (1,)), ((), ()))

    @pl.loop(0, nb)
    def _(step):
        b = lax.rem(my_b + step, nb)
        pltpu.make_async_copy(recv_a.at[b], recv_a.at[b], recv_a_sem.at[b]).wait()
        data = recv_a[b].reshape(nf * part, LANES)
        acc[...] += lax.dot_general(table[b], data, across_rows, preferred_element_type=jnp.float32)

    per_c = nf * pack // 2
    group = [acc[(g % pack) * total : (g % pack + 1) * total, (g // pack) * part : (g // pack + 1) * part]
             for g in range(nf * pack)]
    direct = jnp.concatenate(
        [jnp.concatenate(group[c * per_c : (c + 1) * per_c], axis=1) for c in range(2)], axis=0
    )
    exact = dict(preferred_element_type=jnp.float32, precision=lax.Precision.HIGHEST)
    modes = lax.dot_general(direct, proj[...], across_rows, **exact) * gamma
    solved = lax.dot_general(modes, recon[...], across_rows, **exact) * keep

    def piece(g):
        c, l = g // per_c, (g % per_c) * part
        return solved[c * total : (c + 1) * total, l : l + part]

    packed = jnp.concatenate(
        [jnp.concatenate([piece(f * pack + h) for f in range(nf)], axis=1) for h in range(pack)], axis=0
    ).T.astype(jnp.bfloat16)

    @pl.loop(0, nb, unroll=UNROLL)
    def _(b):
        got = jnp.dot(packed, table[b], preferred_element_type=jnp.float32)
        send_b[pl.ds(b * nf, nf)] = got.astype(jnp.bfloat16).reshape(nf, part, LANES)

    @pl.loop(1, n_dev, unroll=UNROLL)
    def _(step):
        other, where = peer(step)
        pltpu.make_async_remote_copy(
            src_ref=send_b.at[other],
            dst_ref=recv_b.at[me],
            send_sem=send_b_sem,
            recv_sem=recv_b_sem,
            device_id=where,
            device_id_type=MESH,
        ).start()

    pltpu.make_async_copy(send_b.at[me], recv_b.at[me], recv_b_sem).start()
    spec_v[...] = solved.astype(jnp.bfloat16).reshape(1, 2, total, LEV)
    spec_out = pltpu.make_async_copy(spec_v, spec_ref, small_sem.at[0])
    spec_out.start()
    pltpu.make_async_copy(recv_b, recv_b, recv_b_sem).wait()

    size = n_dev // CHUNKS
    outs = []
    for k in range(CHUNKS):
        @pl.loop(k * size, (k + 1) * size, unroll=UNROLL)
        def _(w):
            x = recv_b[jnp.clip(order[0, w], 0, n_dev - 1)].astype(jnp.float32)
            for h in range(pack):
                out_v[w, h * part : (h + 1) * part, :] = x[:, h * width : (h + 1) * width].astype(jnp.bfloat16)
        span = pl.ds(k * size, size)
        outs.append(pltpu.make_async_copy(out_v.at[span], out_ref.at[span], out_sem.at[k]))
        outs[-1].start()

    spec_out.wait()
    others = pl.ds(0, n_dev - 1)
    pltpu.make_async_copy(send_a.at[others], send_a.at[others], send_a_sem).wait()
    pltpu.make_async_copy(send_b.at[others], send_b.at[others], send_b_sem).wait()
    for out in outs:
        out.wait()


def per_device(fourier, quad_weights, legendre, slot_wave, vert_proj, vert_recon, vert_rates):
    nb, nf = lax.axis_size("band"), lax.axis_size("field")
    n_dev = nb * nf
    waves, rows, width = fourier.shape
    per_dev, nlat, total = legendre.shape
    assert per_dev == 1 and waves == n_dev and nlat == nb * width and width <= LANES
    pack = 1
    while rows % (2 * pack * 8) == 0 and 2 * pack * width <= LANES and 2 * pack * total <= LANES:
        pack *= 2
    part = rows // pack
    wide = -(-n_dev // LANES) * LANES
    anywhere = pl.BlockSpec(memory_space=pl.ANY)
    blocks = (n_dev, part, LANES)
    leg = legendre.transpose(0, 2, 1)
    dma = pltpu.SemaphoreType.DMA
    spec, returned = pl.pallas_call(
        functools.partial(exchange, nb, nf, pack),
        out_shape=(
            jax.ShapeDtypeStruct((1, 2, total, LEV), jnp.bfloat16),
            jax.ShapeDtypeStruct(fourier.shape, jnp.bfloat16),
        ),
        in_specs=[anywhere] * 8,
        out_specs=(anywhere, anywhere),
        scratch_shapes=[
            pltpu.SMEM((n_dev,), jnp.int32),
            pltpu.SMEM((1, wide), jnp.int32),
            pltpu.VMEM((1, n_dev), jnp.int32),
            pltpu.VMEM((1, width), jnp.float32),
            pltpu.VMEM((1, LEV), jnp.float32),
            pltpu.VMEM(leg.shape, jnp.bfloat16),
            pltpu.VMEM((LEV, LEV), jnp.float32),
            pltpu.VMEM((LEV, LEV), jnp.float32),
            pltpu.VMEM(fourier.shape, jnp.bfloat16),
            pltpu.VMEM(blocks, jnp.bfloat16),
            pltpu.VMEM((nb, nf, part, LANES), jnp.bfloat16),
            pltpu.VMEM(blocks, jnp.bfloat16),
            pltpu.VMEM(blocks, jnp.bfloat16),
            pltpu.VMEM((nb, pack * total, LANES), jnp.bfloat16),
            pltpu.VMEM((pack * total, nf * part), jnp.float32),
            pltpu.VMEM((1, wide), jnp.int32),
            pltpu.VMEM((1, 2, total, LEV), jnp.bfloat16),
            pltpu.VMEM(fourier.shape, jnp.bfloat16),
            dma((7,)),
            dma,
            dma((CHUNKS,)),
            dma,
            dma((nb,)),
            dma,
            dma,
        ],
        compiler_params=pltpu.CompilerParams(
            collective_id=0, has_side_effects=True, vmem_limit_bytes=VMEM_LIMIT
        ),
    )(slot_wave, slot_wave[None], quad_weights[None], vert_rates[None], leg, vert_proj, vert_recon, fourier)
    return spec.transpose(0, 1, 3, 2), returned


def solution(mesh):
    placed = (
        P(None, "field", "band"),
        P("band"),
        P(("band", "field"), None, None),
        P(),
        P(),
        P(),
        P(),
    )
    return jax.shard_map(
        per_device,
        mesh=mesh,
        in_specs=placed,
        out_specs=(P(("band", "field"), None, None, None), P(None, "field", "band")),
        check_vma=False,
    )
```

time: 32.4 us -> 27.4 us (0.85)
  Pallas kernels: 28.5 us -> 23.4 us
    pallas_call x1 -> x0, Pallas kernels: 3.97 us -> none  [per_device(): pl.pallas_call(functools.partial(unpack, pack), out_shape=(jax.ShapeDtype...]
    unnamed x1 -> x2, local copies, waits for them, and re-layouts: 1.52 us -> 3.09 us
    pallas_call x1 -> x0, local copies, waits for them, and re-layouts: 1.48 us -> none  [per_device(): pl.pallas_call(functools.partial(unpack, pack), out_shape=(jax.ShapeDtype...]
    pallas_call x1, Pallas kernels: 24.5 us -> 23.4 us  [per_device(): pl.pallas_call(functools.partial(exchange, nb, nf, pack), out_shape=(jax....]
where the time goes in v2:
time: 27.4 us; the launch traced here: 27.1 us
  Pallas kernels  23.4 us (85%)
  local copies, waits for them, and re-layouts  3.09 us (11%)
  between operations  0.64 us (2%)
    pallas_call x1, Pallas kernels, per_device(): pl.pallas_call(functools.partial(exchange, nb, nf, pack), out_shape=(jax....  23.4 us
    unnamed x2, local copies, waits for them, and re-layouts  3.09 us

profile of v2, /device:TPU:0, one launch (start us, length us, event | category | flops | bytes accessed | tf_op | source)
XLA Modules:
  0.0 27.1 jit_solution(15478358593260861603)
XLA Ops:
  0.6 23.4 %shard_map.86 = (bf16[1,2,32,96]{3,2,1,0:T(8,128)(2,1)}, bf16[32,48,56]{2,1,0:T(8,128)(2,1)}) custom-call(s32[32]{0:T(128)} %wave_hbm.1, s32[1,32]{1,0:T(1,128)} %bitcast.7, f32[1,56]{1,0:T(1,128)} %bitcast.8, f32[1,96]{1,0:T(1,128)} %bitcast.9, bf16[1,32,448]{2,1,0:T(8,128)(2,1)} %bitcast.5, f32[96,96]{1,0:T(8,128)} %proj_hbm.1, f32[96,96]{1,0:T(8,128)} %recon_hbm.1, ...), custom_call_target="tpu_custom_call" | custom-call | tf_op jit(solution)/shard_map/pallas_call | solution.py:195
  24.0 1.3 %copy.11 = bf16[1,2,96,32]{2,3,1,0:T(8,128)(2,1)} copy(bf16[1,2,96,32]{2,3,1,0:T(8,128)(2,1)} %bitcast.6) | data formatting | bytes 24576
  25.4 1.8 %copy.12 = bf16[32,48,56]{2,1,0:T(8,128)(2,1)} copy(bf16[32,48,56]{2,1,0:T(8,128)(2,1)} %get-tuple-element.9) | data formatting | bytes 344064

commit v3 on v2

--- a/solution.py
+++ b/solution.py
@@ -9,9 +9,9 @@
 
 LEV = 96
 LANES = 128
-UNROLL = 4
-CHUNKS = 4
-VMEM_LIMIT = 60 * 1024 * 1024
+UNROLL = 8
+UNROLL_PEERS = 7
+VMEM_LIMIT = 40 * 1024 * 1024
 MESH = pl.DeviceIdType.MESH
 
 
@@ -19,8 +19,8 @@
     nb, nf, pack, wave_hbm, row_hbm, quad_hbm, rates_hbm, leg_hbm, proj_hbm, recon_hbm, fourier_hbm,
     spec_ref, out_ref,
     wave, order, row, quad, rates, leg, proj, recon, four, send_a, recv_a, send_b, recv_b, table, acc,
-    inverse_v, spec_v, out_v,
-    small_sem, four_sem, out_sem, send_a_sem, recv_a_sem, send_b_sem, recv_b_sem,
+    inverse_v,
+    small_sem, four_sem, send_a_sem, recv_a_sem, send_b_sem, recv_b_sem,
 ):
     n_dev = nb * nf
     my_b, my_f = lax.axis_index("band"), lax.axis_index("field")
@@ -29,15 +29,27 @@
     part = rows // pack
     total = leg.shape[1]
 
-    def peer(step):
-        other = lax.rem(me + step, n_dev)
-        return other, (other // nf, lax.rem(other, nf))
+    def wrap(at, size):
+        return jnp.where(at >= size, at - size, at)
+
+    fields = [wrap(my_f + step, nf) for step in range(nf)]
+
+    def each_peer(act):
+        for f in fields[1:]:
+            act(me - my_f + f, (my_b, f))
+
+        @pl.loop(1, nb, unroll=UNROLL_PEERS)
+        def _(step):
+            b = wrap(my_b + step, nb)
+            for f in fields:
+                act(b * nf + f, (b, f))
 
     barrier = pltpu.get_barrier_semaphore()
 
-    @pl.loop(1, n_dev, unroll=UNROLL)
-    def _(step):
-        pl.semaphore_signal(barrier, inc=1, device_id=peer(step)[1], device_id_type=MESH)
+    def greet(other, where):
+        pl.semaphore_signal(barrier, inc=1, device_id=where, device_id_type=MESH)
+
+    each_peer(greet)
 
     pairs = ((wave_hbm, wave), (quad_hbm, quad), (row_hbm, row), (leg_hbm, leg), (rates_hbm, rates),
              (proj_hbm, proj), (recon_hbm, recon))
@@ -61,9 +73,7 @@
 
     pl.semaphore_wait(barrier, n_dev - 1)
 
-    @pl.loop(1, n_dev, unroll=UNROLL)
-    def _(step):
-        other, where = peer(step)
+    def forward(other, where):
         pltpu.make_async_remote_copy(
             src_ref=send_a.at[other],
             dst_ref=recv_a.at[my_b, my_f],
@@ -73,6 +83,7 @@
             device_id_type=MESH,
         ).start()
 
+    each_peer(forward)
     pltpu.make_async_copy(send_a.at[me], recv_a.at[my_b, my_f], recv_a_sem.at[my_b]).start()
 
     loads[2].wait()
@@ -111,7 +122,7 @@
 
     @pl.loop(0, nb)
     def _(step):
-        b = lax.rem(my_b + step, nb)
+        b = wrap(my_b + nb - step, nb)
         pltpu.make_async_copy(recv_a.at[b], recv_a.at[b], recv_a_sem.at[b]).wait()
         data = recv_a[b].reshape(nf * part, LANES)
         acc[...] += lax.dot_general(table[b], data, across_rows, preferred_element_type=jnp.float32)
@@ -134,47 +145,44 @@
         [jnp.concatenate([piece(f * pack + h) for f in range(nf)], axis=1) for h in range(pack)], axis=0
     ).T.astype(jnp.bfloat16)
 
-    @pl.loop(0, nb, unroll=UNROLL)
-    def _(b):
+    def synthesize(b):
         got = jnp.dot(packed, table[b], preferred_element_type=jnp.float32)
         send_b[pl.ds(b * nf, nf)] = got.astype(jnp.bfloat16).reshape(nf, part, LANES)
 
-    @pl.loop(1, n_dev, unroll=UNROLL)
-    def _(step):
-        other, where = peer(step)
+    def backward(b, f):
+        other = b * nf + f
         pltpu.make_async_remote_copy(
             src_ref=send_b.at[other],
             dst_ref=recv_b.at[me],
             send_sem=send_b_sem,
             recv_sem=recv_b_sem,
-            device_id=where,
+            device_id=(b, f),
             device_id_type=MESH,
         ).start()
 
+    synthesize(wrap(my_b + 1, nb))
+
+    @pl.loop(1, nb, unroll=UNROLL_PEERS)
+    def _(step):
+        synthesize(wrap(my_b + step + 1, nb))
+        for f in fields:
+            backward(wrap(my_b + step, nb), f)
+
+    for f in fields[1:]:
+        backward(my_b, f)
     pltpu.make_async_copy(send_b.at[me], recv_b.at[me], recv_b_sem).start()
-    spec_v[...] = solved.astype(jnp.bfloat16).reshape(1, 2, total, LEV)
-    spec_out = pltpu.make_async_copy(spec_v, spec_ref, small_sem.at[0])
-    spec_out.start()
+    spec_ref[...] = solved.astype(jnp.bfloat16).reshape(1, 2, total, LEV)
     pltpu.make_async_copy(recv_b, recv_b, recv_b_sem).wait()
 
-    size = n_dev // CHUNKS
-    outs = []
-    for k in range(CHUNKS):
-        @pl.loop(k * size, (k + 1) * size, unroll=UNROLL)
-        def _(w):
-            x = recv_b[jnp.clip(order[0, w], 0, n_dev - 1)].astype(jnp.float32)
-            for h in range(pack):
-                out_v[w, h * part : (h + 1) * part, :] = x[:, h * width : (h + 1) * width].astype(jnp.bfloat16)
-        span = pl.ds(k * size, size)
-        outs.append(pltpu.make_async_copy(out_v.at[span], out_ref.at[span], out_sem.at[k]))
-        outs[-1].start()
-
-    spec_out.wait()
+    @pl.loop(0, n_dev, unroll=UNROLL)
+    def _(w):
+        x = recv_b[jnp.clip(order[0, w], 0, n_dev - 1)].astype(jnp.float32)
+        for h in range(pack):
+            out_ref[w, h * part : (h + 1) * part, :] = x[:, h * width : (h + 1) * width].astype(jnp.bfloat16)
+
     others = pl.ds(0, n_dev - 1)
     pltpu.make_async_copy(send_a.at[others], send_a.at[others], send_a_sem).wait()
     pltpu.make_async_copy(send_b.at[others], send_b.at[others], send_b_sem).wait()
-    for out in outs:
-        out.wait()
 
 
 def per_device(fourier, quad_weights, legendre, slot_wave, vert_proj, vert_recon, vert_rates):
@@ -199,7 +207,7 @@
             jax.ShapeDtypeStruct(fourier.shape, jnp.bfloat16),
         ),
         in_specs=[anywhere] * 8,
-        out_specs=(anywhere, anywhere),
+        out_specs=(pl.BlockSpec(memory_space=pltpu.VMEM),) * 2,
         scratch_shapes=[
             pltpu.SMEM((n_dev,), jnp.int32),
             pltpu.SMEM((1, wide), jnp.int32),
@@ -217,11 +225,8 @@
             pltpu.VMEM((nb, pack * total, LANES), jnp.bfloat16),
             pltpu.VMEM((pack * total, nf * part), jnp.float32),
             pltpu.VMEM((1, wide), jnp.int32),
-            pltpu.VMEM((1, 2, total, LEV), jnp.bfloat16),
-            pltpu.VMEM(fourier.shape, jnp.bfloat16),
             dma((7,)),
             dma,
-            dma((CHUNKS,)),
             dma,
             dma((nb,)),
             dma,
@@ -230,7 +235,7 @@
         compiler_params=pltpu.CompilerParams(
             collective_id=0, has_side_effects=True, vmem_limit_bytes=VMEM_LIMIT
         ),
-    )(slot_wave, slot_wave[None], quad_weights[None], vert_rates[None], leg, vert_proj, vert_recon, fourier)
+    )(*[pltpu.with_memory_space_constraint(a, pltpu.HBM) for a in (slot_wave, slot_wave[None], quad_weights[None], vert_rates[None], leg, vert_proj, vert_recon, fourier)])
     return spec.transpose(0, 1, 3, 2), returned
 
 

time: 27.4 us -> 23.4 us (0.85)
  Pallas kernels: 23.4 us -> 21.2 us
  local copies, waits for them, and re-layouts: 3.09 us -> 1.35 us
    pallas_call x1, Pallas kernels: 23.4 us -> 21.2 us  [per_device(): pl.pallas_call(functools.partial(exchange, nb, nf, pack), out_shape=(jax....]
    unnamed x2, local copies, waits for them, and re-layouts: 3.09 us -> 1.35 us
where the time goes in v3:
time: 23.4 us; the launch traced here: 23.2 us
  Pallas kernels  21.2 us (91%)
  local copies, waits for them, and re-layouts  1.35 us (6%)
  between operations  0.64 us (3%)
    pallas_call x1, Pallas kernels, per_device(): pl.pallas_call(functools.partial(exchange, nb, nf, pack), out_shape=(jax....  21.2 us
    unnamed x2, local copies, waits for them, and re-layouts  1.35 us

profile of v3, /device:TPU:0, one launch (start us, length us, event | category | flops | bytes accessed | tf_op | source)
XLA Modules:
  0.0 23.2 jit_solution(7515498547826877319)
XLA Ops:
  0.6 21.2 %shard_map.86 = (bf16[1,2,32,96]{3,2,1,0:T(8,128)(2,1)S(1)}, bf16[32,48,56]{2,1,0:T(8,128)(2,1)S(1)}) custom-call(s32[32]{0:T(128)} %wave_hbm.1, s32[1,32]{1,0:T(1,128)} %bitcast.7, f32[1,56]{1,0:T(1,128)} %bitcast.8, f32[1,96]{1,0:T(1,128)} %bitcast.9, bf16[1,32,448]{2,1,0:T(8,128)(2,1)} %bitcast.6, f32[96,96]{1,0:T(8,128)} %proj_hbm.1, ...), custom_call_target="tpu_custom_call" | custom-call | tf_op jit(solution)/shard_map/pallas_call | solution.py:203
  21.9 0.6 %copy.11 = bf16[1,2,96,32]{2,3,1,0:T(8,128)(2,1)} copy(bf16[1,2,96,32]{2,3,1,0:T(8,128)(2,1)S(1)} %bitcast.5) | data formatting | bytes 24576
  22.5 0.7 %copy.12 = bf16[32,48,56]{2,1,0:T(8,128)(2,1)} copy(bf16[32,48,56]{2,1,0:T(8,128)(2,1)S(1)} %get-tuple-element.9) | data formatting | bytes 344064

commit v4 on v3

--- a/solution.py
+++ b/solution.py
@@ -40,7 +40,7 @@
 
         @pl.loop(1, nb, unroll=UNROLL_PEERS)
         def _(step):
-            b = wrap(my_b + step, nb)
+            b = lax.rem(my_b + nb - step, nb)
             for f in fields:
                 act(b * nf + f, (b, f))
 
@@ -122,7 +122,7 @@
 
     @pl.loop(0, nb)
     def _(step):
-        b = wrap(my_b + nb - step, nb)
+        b = wrap(my_b + step, nb)
         pltpu.make_async_copy(recv_a.at[b], recv_a.at[b], recv_a_sem.at[b]).wait()
         data = recv_a[b].reshape(nf * part, LANES)
         acc[...] += lax.dot_general(table[b], data, across_rows, preferred_element_type=jnp.float32)
@@ -160,13 +160,13 @@
             device_id_type=MESH,
         ).start()
 
-    synthesize(wrap(my_b + 1, nb))
+    synthesize(lax.rem(my_b + nb - 1, nb))
 
     @pl.loop(1, nb, unroll=UNROLL_PEERS)
     def _(step):
-        synthesize(wrap(my_b + step + 1, nb))
+        synthesize(lax.rem(my_b + nb + nb - step - 1, nb))
         for f in fields:
-            backward(wrap(my_b + step, nb), f)
+            backward(lax.rem(my_b + nb - step, nb), f)
 
     for f in fields[1:]:
         backward(my_b, f)
@@ -183,6 +183,17 @@
     others = pl.ds(0, n_dev - 1)
     pltpu.make_async_copy(send_a.at[others], send_a.at[others], send_a_sem).wait()
     pltpu.make_async_copy(send_b.at[others], send_b.at[others], send_b_sem).wait()
+
+
+def hand_over(spec_in, grid_in, spec_out, grid_out, sems):
+    copies = [
+        pltpu.make_async_copy(grid_in, grid_out, sems.at[0]),
+        pltpu.make_async_copy(spec_in, spec_out, sems.at[1]),
+    ]
+    for copy in copies:
+        copy.start()
+    for copy in copies:
+        copy.wait()
 
 
 def per_device(fourier, quad_weights, legendre, slot_wave, vert_proj, vert_recon, vert_rates):
@@ -236,6 +247,17 @@
             collective_id=0, has_side_effects=True, vmem_limit_bytes=VMEM_LIMIT
         ),
     )(*[pltpu.with_memory_space_constraint(a, pltpu.HBM) for a in (slot_wave, slot_wave[None], quad_weights[None], vert_rates[None], leg, vert_proj, vert_recon, fourier)])
+    spec, returned = pl.pallas_call(
+        hand_over,
+        out_shape=(
+            jax.ShapeDtypeStruct(spec.shape, spec.dtype),
+            jax.ShapeDtypeStruct(returned.shape, returned.dtype),
+        ),
+        in_specs=[anywhere] * 2,
+        out_specs=(anywhere, anywhere),
+        scratch_shapes=[dma((2,))],
+        compiler_params=pltpu.CompilerParams(vmem_limit_bytes=VMEM_LIMIT),
+    )(spec, returned)
     return spec.transpose(0, 1, 3, 2), returned
 
 

time: 23.4 us -> 22.6 us (0.966)
  local copies, waits for them, and re-layouts: 1.35 us -> 0 us
  Pallas kernels: 21.2 us -> 21.8 us
    unnamed x2 -> x0, local copies, waits for them, and re-layouts: 1.35 us -> none
    pallas_call x0 -> x1, Pallas kernels: none -> 0.77 us  [per_device(): pl.pallas_call(hand_over, out_shape=(jax.ShapeDtypeStruct(spec.shape, spe...]
where the time goes in v4:
time: 22.6 us; the launch traced here: 22.4 us
  Pallas kernels  21.8 us (96%)
  between operations  0.64 us (3%)
    pallas_call x1, Pallas kernels, per_device(): pl.pallas_call(functools.partial(exchange, nb, nf, pack), out_shape=(jax....  21 us
    pallas_call x1, Pallas kernels, per_device(): pl.pallas_call(hand_over, out_shape=(jax.ShapeDtypeStruct(spec.shape, spe...  0.77 us

profile of v4, /device:TPU:0, one launch (start us, length us, event | category | flops | bytes accessed | tf_op | source)
XLA Modules:
  0.0 22.4 jit_solution(5574658989514823027)
XLA Ops:
  0.6 21.0 %shard_map.86 = (bf16[1,2,32,96]{3,2,1,0:T(8,128)(2,1)S(1)}, bf16[32,48,56]{2,1,0:T(8,128)(2,1)S(1)}) custom-call(s32[32]{0:T(128)} %wave_hbm.1, s32[1,32]{1,0:T(1,128)} %bitcast.6, f32[1,56]{1,0:T(1,128)} %bitcast.7, f32[1,96]{1,0:T(1,128)} %bitcast.8, bf16[1,32,448]{2,1,0:T(8,128)(2,1)} %bitcast.5, f32[96,96]{1,0:T(8,128)} %proj_hbm.1, ...), custom_call_target="tpu_custom_call" | custom-call | tf_op jit(solution)/shard_map/pallas_call | solution.py:214
  21.7 0.8 %shard_map.87 = (bf16[1,2,32,96]{3,2,1,0:T(8,128)(2,1)}, bf16[32,48,56]{2,1,0:T(8,128)(2,1)}) custom-call(bf16[1,2,32,96]{3,2,1,0:T(8,128)(2,1)S(1)} %get-tuple-element.6.spec_in, bf16[32,48,56]{2,1,0:T(8,128)(2,1)S(1)} %get-tuple-element.7.grid_in), custom_call_target="tpu_custom_call" | custom-call | tf_op jit(solution)/shard_map/pallas_call | solution.py:250

commit v5 on v4

--- a/solution.py
+++ b/solution.py
@@ -9,7 +9,7 @@
 
 LEV = 96
 LANES = 128
-UNROLL = 8
+UNROLL = 16
 UNROLL_PEERS = 7
 VMEM_LIMIT = 40 * 1024 * 1024
 MESH = pl.DeviceIdType.MESH

time: 22.6 us -> 22.4 us (level)
  no operation moved by 1% of the time
where the time goes in v5:
time: 22.4 us; the launch traced here: 22.3 us
  Pallas kernels  21.6 us (96%)
  between operations  0.64 us (3%)
    pallas_call x1, Pallas kernels, per_device(): pl.pallas_call(functools.partial(exchange, nb, nf, pack), out_shape=(jax....  20.9 us
    pallas_call x1, Pallas kernels, per_device(): pl.pallas_call(hand_over, out_shape=(jax.ShapeDtypeStruct(spec.shape, spe...  0.77 us

profile of v5, /device:TPU:0, one launch (start us, length us, event | category | flops | bytes accessed | tf_op | source)
XLA Modules:
  0.0 22.3 jit_solution(4543836907491104522)
XLA Ops:
  0.6 20.9 %shard_map.86 = (bf16[1,2,32,96]{3,2,1,0:T(8,128)(2,1)S(1)}, bf16[32,48,56]{2,1,0:T(8,128)(2,1)S(1)}) custom-call(s32[32]{0:T(128)} %wave_hbm.1, s32[1,32]{1,0:T(1,128)} %bitcast.6, f32[1,56]{1,0:T(1,128)} %bitcast.7, f32[1,96]{1,0:T(1,128)} %bitcast.8, bf16[1,32,448]{2,1,0:T(8,128)(2,1)} %bitcast.5, f32[96,96]{1,0:T(8,128)} %proj_hbm.1, ...), custom_call_target="tpu_custom_call" | custom-call | tf_op jit(solution)/shard_map/pallas_call | solution.py:214
  21.5 0.8 %shard_map.87 = (bf16[1,2,32,96]{3,2,1,0:T(8,128)(2,1)}, bf16[32,48,56]{2,1,0:T(8,128)(2,1)}) custom-call(bf16[1,2,32,96]{3,2,1,0:T(8,128)(2,1)S(1)} %get-tuple-element.6.spec_in, bf16[32,48,56]{2,1,0:T(8,128)(2,1)S(1)} %get-tuple-element.7.grid_in), custom_call_target="tpu_custom_call" | custom-call | tf_op jit(solution)/shard_map/pallas_call | solution.py:250
